TPU v7x, 32 devices: a whole 2x2x4 slice. The times are simulated.
32 devices in a mesh: graph: 8 (over z, y), member: 4 (over x, core).
Axes of the slice: x: 2, y: 2, z: 4, core: 2. Of those that a mesh axis runs over, the one named last changes fastest.
Arguments:
- node_latents: bfloat16 [16, 1024, 512], P('member', 'graph'), may hold values from -6 to 6
- edge_latents: bfloat16 [6144, 512], P('graph'), may hold values from -6 to 6
- neighbours: int32 [8, 4], P('graph'), may hold values from 0 to 7, as said below
- edge_source: int32 [8, 768], P('graph'), may hold values from 0 to 639, as said below
- edge_dest: int32 [8, 768], P('graph'), may hold values from 0 to 127, as said below
- edge_count: int32 [8], P('graph'), may hold values from 153 to 768, as said below
- edge_in: bfloat16 [1, 3, 512, 512], replicated, may hold values from -0.15625 to 0.15625
- edge_out: bfloat16 [1, 512, 512], replicated, may hold values from -0.25 to 0.25
- node_in: bfloat16 [1, 2, 512, 512], replicated, may hold values from -0.1875 to 0.1875
- node_out: bfloat16 [1, 512, 512], replicated, may hold values from -0.25 to 0.25
- biases: float32 [1, 4, 512], replicated, may hold values from -3 to 3
- gains: float32 [1, 2, 512], replicated, may hold values from 0.25 to 1.75
Outputs:
- ens_mean: bfloat16 [1024, 512], P('graph')
- ens_spread: bfloat16 [1024, 512], P('graph')
Inputs may be any that keep to these rules, and one draw needn't show every extreme that they name: `neighbours`: row b lists 4 distinct blocks other than b, each within 3 blocks of b along the closed order of blocks (numbers taken modulo 8). `edge_source`: among the live edge slots of one block, at most 32 distinct sender nodes lie in any one listed block, and exactly 32 in one of them. `edge_dest`: every node receives at least one live edge slot of its block. `edge_count`: some block has all 768 slots live.
All inputs are finite; a program needn't handle non-finite values.
Results may differ from a plain program's by a relative error of at most 0.006.
Values may be sent and summed in bfloat16 or wider, within the bound.
A program may use at most 64 MiB of HBM per device.

v0:
```python
import jax
import jax.numpy as jnp
from jax import lax
from jax.sharding import PartitionSpec as P

RADIUS = 3


def from_behind(value, axis, steps):
    count = lax.axis_size(axis)
    pairs = [(source, (source + steps) % count) for source in range(count)]
    return lax.ppermute(value, axis, pairs)


def layer_norm(values, gain):
    centre = jnp.mean(values, axis=-1, keepdims=True)
    centered = values - centre
    variance = jnp.mean(centered * centered, axis=-1, keepdims=True)
    return centered * lax.rsqrt(variance + 1e-05) * gain


def fetch_block(sender_proj, offset):
    return from_behind(sender_proj, "graph", offset)


def edge_update(
    state_rows, sender_rows, dest_rows, dest_hot, weight_in, weight_out, bias_rows, gain
):
    edge_proj = jnp.dot(state_rows, weight_in, preferred_element_type=jnp.float32)[None]
    hidden = edge_proj + sender_rows.astype(jnp.float32) + dest_rows + bias_rows[0]
    activated = jax.nn.silu(hidden).astype(jnp.bfloat16)
    mixed = (
        jnp.einsum("mel,lk->mek", activated, weight_out, preferred_element_type=jnp.float32)
        + bias_rows[1]
    )
    updated = (state_rows.astype(jnp.float32) + layer_norm(mixed, gain)).astype(jnp.bfloat16)
    partial_sum = jnp.einsum("en,mel->mnl", dest_hot, updated, preferred_element_type=jnp.float32)
    return (updated, partial_sum)


def local(
    node_latents,
    edge_latents,
    neighbours,
    edge_source,
    edge_dest,
    edge_count,
    edge_in,
    edge_out,
    node_in,
    node_out,
    biases,
    gains,
):
    members, block_rows, latent_width = node_latents.shape
    edge_slots = edge_source.shape[1]
    nbr_count = neighbours.shape[1]
    groups = lax.axis_size("graph")
    own_index = lax.axis_index("graph")
    offsets = [reach_by for reach_by in range(1, RADIUS + 1)] + [
        -reach_by for reach_by in range(1, RADIUS + 1)
    ]
    src_slot = edge_source[0] // block_rows
    src_node = edge_source[0] % block_rows
    dst_node = edge_dest[0]
    is_live = jnp.arange(edge_slots, dtype=jnp.int32) < edge_count[0]
    distance = (own_index - neighbours[0]) % groups
    signed = jnp.where(distance > groups // 2, distance - groups, distance)
    position = jnp.where(signed > 0, signed - 1, RADIUS - signed - 1)
    slot_ids = jnp.arange(nbr_count, dtype=jnp.int32)
    slot_match = src_slot[:, None] == slot_ids[None, :]
    slot_position = jnp.sum(jnp.where(slot_match, position[None, :], 0), axis=1)
    is_own = src_slot == nbr_count
    node_ids = jnp.arange(block_rows, dtype=jnp.int32)
    row_index = jnp.where(is_own, src_node, block_rows * (1 + slot_position) + src_node)
    dest_hot = ((dst_node[:, None] == node_ids[None, :]) & is_live[:, None]).astype(jnp.bfloat16)
    edge_state = edge_latents
    state = node_latents
    edge_weights = edge_in[0]
    sender_proj = jnp.einsum(
        "mnl,lk->mnk", state, edge_weights[1], preferred_element_type=jnp.float32
    ).astype(jnp.bfloat16)
    receiver_proj = jnp.einsum(
        "mnl,lk->mnk", state, edge_weights[2], preferred_element_type=jnp.float32
    )
    pieces = [sender_proj] + [fetch_block(sender_proj, reach_by) for reach_by in offsets]
    row_table = jnp.concatenate(pieces, axis=1)
    senders = jnp.take(row_table, row_index, axis=1)
    dest_proj = jnp.take(receiver_proj, dst_node, axis=1)
    edge_state, total = edge_update(
        edge_state,
        senders,
        dest_proj,
        dest_hot,
        edge_weights[0],
        edge_out[0],
        biases[0],
        gains[0, 0],
    )
    gathered = total.astype(jnp.bfloat16)
    node_weights = node_in[0]
    node_hidden = jnp.einsum(
        "mnl,lk->mnk", state, node_weights[0], preferred_element_type=jnp.float32
    )
    node_hidden = (
        node_hidden
        + jnp.einsum("mnl,lk->mnk", gathered, node_weights[1], preferred_element_type=jnp.float32)
        + biases[0, 2]
    )
    node_act = jax.nn.silu(node_hidden).astype(jnp.bfloat16)
    node_mixed = (
        jnp.einsum("mnl,lk->mnk", node_act, node_out[0], preferred_element_type=jnp.float32)
        + biases[0, 3]
    )
    state = (state.astype(jnp.float32) + layer_norm(node_mixed, gains[0, 1])).astype(jnp.bfloat16)
    finals = state.astype(jnp.float32)
    ensemble = members * lax.axis_size("member")
    total_state, squares = lax.psum(
        (jnp.sum(finals, axis=0), jnp.sum(finals * finals, axis=0)), "member"
    )
    centre = total_state / ensemble
    spread = jnp.sqrt(squares / ensemble - centre * centre)
    return (centre.astype(jnp.bfloat16), spread.astype(jnp.bfloat16))


def solution(mesh):
    return jax.shard_map(
        local,
        mesh=mesh,
        in_specs=(
            P("member", "graph", None),
            P("graph", None),
            P("graph", None),
            P("graph", None),
            P("graph", None),
            P("graph"),
            P(),
            P(),
            P(),
            P(),
            P(),
            P(),
        ),
        out_specs=(P("graph", None), P("graph", None)),
        check_vma=False,
    )
```

profile of v0, /device:TPU:5, one launch (start us, length us, event | category | flops | bytes accessed | tf_op | source)
XLA Modules:
  0.0 160.2 jit_solution(7688985698605042821)
XLA Ops:
  7.3 2.7 %constant_dynamic-update-slice_fusion.6 = (bf16[4,896,512]{2,1,0:T(8,128)(2,1)}, bf16[4,128,512]{2,1,0:T(8,128)(2,1)}) fusion(bf16[4,128,512]{2,1,0:T(8,128)(2,1)} %param.12, bf16[1,3,512,512]{3,2,1,0:T(8,128)(2,1)} %param.18), kind=kOutput, calls=%fused_computation.62 | convolution fusion | flops 268697600 | bytes 2097152 | tf_op jit(solution)/shard_map/mnl,lk->mnk/dot_general | solution.py:80
  10.0 1.2 collective-permute-start
  11.3 1.3 collective-permute-start.1
  12.6 2.3 %collective-permute-start.2 = (bf16[4,128,512]{2,1,0:T(8,128)(2,1)}, bf16[4,128,512]{2,1,0:T(8,128)(2,1)}, u32[]{:S(2)}, u32[]{:S(2)}) collective-permute-start(bf16[4,128,512]{2,1,0:T(8,128)(2,1)} %get-tuple-element.15), channel_id=1, source_target_pairs={{0,12},{4,16},{8,20},{12,24},{16,28},{20,0},{24,4},{28,8},{1,13},{... | collective-permute-start | bytes 1572872 | tf_op jit(solution)/shard_map/ppermute | solution.py:12
  15.0 2.0 %collective-permute-start.4 = (bf16[4,128,512]{2,1,0:T(8,128)(2,1)}, bf16[4,128,512]{2,1,0:T(8,128)(2,1)}, u32[]{:S(2)}, u32[]{:S(2)}) collective-permute-start(bf16[4,128,512]{2,1,0:T(8,128)(2,1)} %get-tuple-element.15), channel_id=1, source_target_pairs={{0,24},{4,28},{8,0},{12,4},{16,8},{20,12},{24,16},{28,20},{1,25},{... | collective-permute-start | bytes 1572872 | tf_op jit(solution)/shard_map/ppermute | solution.py:12
  17.0 1.6 %fusion.17 = f32[4,128,512]{2,1,0:T(8,128)S(1)} fusion(bf16[4,128,512]{2,1,0:T(8,128)(2,1)} %param.12, bf16[1,3,512,512]{3,2,1,0:T(8,128)(2,1)} %param.18), kind=kOutput, calls=%fused_computation.32 | convolution fusion | flops 268435456 | bytes 2097152 | tf_op jit(solution)/shard_map/mnl,lk->mnk/dot_general | solution.py:83
  18.9 2.8 %fusion.23 = f32[768,512]{1,0:T(8,128)} fusion(bf16[768,512]{1,0:T(8,128)(2,1)S(1)} %copy-done.2, bf16[1,3,512,512]{3,2,1,0:T(8,128)(2,1)} %param.18), kind=kOutput, calls=%fused_computation.38 | convolution fusion | flops 402653184 | bytes 2883584 | tf_op jit(solution)/shard_map/dot_general | solution.py:29
  21.7 2.5 %fusion.20 = f32[4,128,512]{2,1,0:T(8,128)} fusion(bf16[4,128,512]{2,1,0:T(8,128)(2,1)S(1)} %copy-done.1, bf16[1,2,512,512]{3,2,1,0:T(8,128)(2,1)} %param.20), kind=kOutput, calls=%fused_computation.35 | convolution fusion | flops 268435456 | bytes 2097152 | tf_op jit(solution)/shard_map/mnl,lk->mnk/dot_general | solution.py:102
  24.9 1.4 copy.27
  26.3 0.7 copy.30
  27.0 6.0 %gather_fusion.1 = f32[768,4,512]{2,1,0:T(4,128)} fusion(f32[4,128,512]{2,0,1:T(4,128)S(1)} %copy.30, s32[1024]{0:T(1024)S(1)} %get-tuple-element.20), kind=kCustom, calls=%fused_computation.1 | custom fusion | bytes 12585984 | tf_op jit(solution)/shard_map/jit(_take)/gather | solution.py:89
  33.1 1.1 collective-permute-start.5
  34.1 1.9 %constant_dynamic-update-slice_fusion.5 = bf16[4,896,512]{2,1,0:T(8,128)(2,1)} fusion(bf16[4,896,512]{2,1,0:T(8,128)(2,1)} %get-tuple-element.14, bf16[4,128,512]{2,1,0:T(8,128)(2,1)} %collective-permute-done), kind=kLoop, calls=%fused_computation.61 | loop fusion | bytes 1048576
  36.1 0.5 collective-permute-done.1
  36.6 1.9 %constant_dynamic-update-slice_fusion.4 = bf16[4,896,512]{2,1,0:T(8,128)(2,1)} fusion(bf16[4,896,512]{2,1,0:T(8,128)(2,1)} %constant_dynamic-update-slice_fusion.5, bf16[4,128,512]{2,1,0:T(8,128)(2,1)} %collective-permute-done.1), kind=kLoop, calls=%fused_computation.60 | loop fusion | bytes 1048576
  38.5 6.2 %collective-permute-done.2 = bf16[4,128,512]{2,1,0:T(8,128)(2,1)} collective-permute-done((bf16[4,128,512]{2,1,0:T(8,128)(2,1)}, bf16[4,128,512]{2,1,0:T(8,128)(2,1)}, u32[]{:S(2)}, u32[]{:S(2)}) %collective-permute-start.2) | collective-permute-done | bytes 524320 | tf_op jit(solution)/shard_map/ppermute | solution.py:12
  44.7 1.9 %constant_dynamic-update-slice_fusion.3 = bf16[4,896,512]{2,1,0:T(8,128)(2,1)} fusion(bf16[4,896,512]{2,1,0:T(8,128)(2,1)} %constant_dynamic-update-slice_fusion.4, bf16[4,128,512]{2,1,0:T(8,128)(2,1)} %collective-permute-done.2), kind=kLoop, calls=%fused_computation.59 | loop fusion | bytes 1048576
  46.6 3.1 %collective-permute-done.3 = bf16[4,128,512]{2,1,0:T(8,128)(2,1)} collective-permute-done((bf16[4,128,512]{2,1,0:T(8,128)(2,1)}, bf16[4,128,512]{2,1,0:T(8,128)(2,1)}, u32[]{:S(2)}, u32[]{:S(2)}) %collective-permute-start.3) | collective-permute-done | bytes 524320 | tf_op jit(solution)/shard_map/ppermute | solution.py:12
  49.7 1.9 %constant_dynamic-update-slice_fusion.2 = bf16[4,896,512]{2,1,0:T(8,128)(2,1)} fusion(bf16[4,896,512]{2,1,0:T(8,128)(2,1)} %constant_dynamic-update-slice_fusion.3, bf16[4,128,512]{2,1,0:T(8,128)(2,1)} %collective-permute-done.3), kind=kLoop, calls=%fused_computation.58 | loop fusion | bytes 1048576
  51.6 4.4 %collective-permute-done.4 = bf16[4,128,512]{2,1,0:T(8,128)(2,1)} collective-permute-done((bf16[4,128,512]{2,1,0:T(8,128)(2,1)}, bf16[4,128,512]{2,1,0:T(8,128)(2,1)}, u32[]{:S(2)}, u32[]{:S(2)}) %collective-permute-start.4) | collective-permute-done | bytes 524320 | tf_op jit(solution)/shard_map/ppermute | solution.py:12
  56.0 1.9 %constant_dynamic-update-slice_fusion.1 = bf16[4,896,512]{2,1,0:T(8,128)(2,1)} fusion(bf16[4,896,512]{2,1,0:T(8,128)(2,1)} %constant_dynamic-update-slice_fusion.2, bf16[4,128,512]{2,1,0:T(8,128)(2,1)} %collective-permute-done.4), kind=kLoop, calls=%fused_computation.57 | loop fusion | bytes 1048576
  57.8 25.5 %collective-permute-done.5 = bf16[4,128,512]{2,1,0:T(8,128)(2,1)S(1)} collective-permute-done((bf16[4,128,512]{2,1,0:T(8,128)(2,1)}, bf16[4,128,512]{2,1,0:T(8,128)(2,1)S(1)}, u32[]{:S(2)}, u32[]{:S(2)}) %collective-permute-start.5) | collective-permute-done | bytes 524320 | tf_op jit(solution)/shard_map/ppermute | solution.py:12
  83.3 0.8 constant_dynamic-update-slice_fusion
  84.2 6.8 %copy.28 = bf16[4,896,512]{2,0,1:T(4,128)(2,1)} copy(bf16[4,896,512]{2,1,0:T(8,128)(2,1)} %constant_dynamic-update-slice_fusion) | data formatting | bytes 7340032 | tf_op jit(solution)/shard_map/concatenate | solution.py:87
  91.0 8.3 %gather_fusion = bf16[768,4,512]{2,1,0:T(4,128)(2,1)} fusion(bf16[4,896,512]{2,0,1:T(4,128)(2,1)} %copy.28, s32[1024]{0:T(1024)S(1)} %get-tuple-element.21), kind=kCustom, calls=%fused_computation | custom fusion | bytes 6294528 | tf_op jit(solution)/shard_map/jit(_take)/gather | solution.py:88
  99.2 8.1 %add_reduce_fusion = (f32[4,768]{1,0:T(4,128)S(1)}, f32[4,768,512]{1,2,0:T(8,128)S(1)}) fusion(f32[512]{0:T(512)S(1)} %bitcast.90, bf16[1,512,512]{2,1,0:T(8,128)(2,1)S(1)} %copy-done, f32[768,4,512]{2,1,0:T(4,128)} %gather_fusion.1, bf16[768,4,512]{2,1,0:T(4,128)(2,1)} %gather_fusion, f32[512]{0:T(512)S(1)} %bitcast.96, f32[768,512]{1,0:T(8,128)S(1)} %copy-done.4, ...), kind=kOutput, calls=%fused_computation.13 | convolution fusion | flops 1631056896 | bytes 17843712 | tf_op jit(solution)/shard_map/mel,lk->mek/dot_general | solution.py:33
  107.4 0.9 multiply_reduce_fusion
  108.8 2.7 %fusion.12 = bf16[4,128,512]{1,2,0:T(8,128)(2,1)} fusion(f32[4,768,512]{1,2,0:T(8,128)S(1)} %get-tuple-element.17, f32[512]{0:T(512)S(1)} %bitcast.93, f32[4,768]{1,0:T(4,128)S(1)} %add_rsqrt_fusion, f32[4,768]{1,0:T(4,128)S(1)} %broadcast_multiply_fusion, f32[512]{0:T(512)S(1)} %bitcast.92, f32[768,512]{0,1:T(8,128)S(1)} %copy-done.3, s32[768]{0:T(1024)S(1)} %reduce.2, ...), kind=kOutput, calls=%fused_computation.25 | convolution fusion | flops 412549120 | bytes 8421120 | tf_op jit(solution)/shard_map/en,mel->mnl/dot_general | solution.py:37
  111.4 2.3 %fusion.50 = (f32[4,128]{1,0:T(4,128)S(1)}, f32[4,128,512]{2,1,0:T(8,128)S(1)}) fusion(f32[512]{0:T(512)S(1)} %bitcast.95, bf16[1,512,512]{2,1,0:T(8,128)(2,1)} %param.21, f32[4,128,512]{2,1,0:T(8,128)S(1)} %copy-done.5, bf16[4,128,512]{1,2,0:T(8,128)(2,1)} %fusion.12, f32[512]{0:T(512)S(1)} %bitcast.94, bf16[1,2,512,512]{3,2,1,0:T(8,128)(2,1)} %param.20), kind=kOutput, calls=%fused_computation.108 | convolution fusion | flops 539229696 | bytes 3676160 | tf_op jit(solution)/shard_map/mnl,lk->mnk/dot_general | solution.py:112
  114.1 1.2 fusion.13
  115.3 36.2 %all-reduce.3.cloned.1.call-done = (f32[128,512]{1,0:T(8,128)}, f32[128,512]{1,0:T(8,128)}) async-done(((f32[128,512]{1,0:T(8,128)}, f32[128,512]{1,0:T(8,128)}), (f32[128,512]{1,0:T(8,128)}, f32[128,512]{1,0:T(8,128)})) %all-reduce.3.cloned.1.call-update) | async-done | bytes 524304 | tf_op jit(solution)/shard_map/psum | solution.py:118
  151.5 1.8 %sqrt_convert_fusion = (bf16[128,512]{1,0:T(8,128)(2,1)}, bf16[128,512]{1,0:T(8,128)(2,1)}) fusion(f32[128,512]{1,0:T(8,128)} %get-tuple-element.5, f32[128,512]{1,0:T(8,128)} %get-tuple-element.4), kind=kLoop, calls=%fused_computation.50 | loop fusion | flops 393216 | bytes 786432 | tf_op jit(solution)/shard_map/convert_element_type | solution.py:123
  (44 shorter events, 1.3 us)
Async XLA Ops:
  7.2 92.1 %copy-start = (bf16[1,512,512]{2,1,0:T(8,128)(2,1)S(1)}, bf16[1,512,512]{2,1,0:T(8,128)(2,1)}, u32[]{:S(2)}) copy-start(bf16[1,512,512]{2,1,0:T(8,128)(2,1)} %param.19) | copy-start | bytes 1572868
  7.2 14.5 %copy-start.1 = (bf16[4,128,512]{2,1,0:T(8,128)(2,1)S(1)}, bf16[4,128,512]{2,1,0:T(8,128)(2,1)}, u32[]{:S(2)}) copy-start(bf16[4,128,512]{2,1,0:T(8,128)(2,1)} %param.12) | copy-start | bytes 1572868
  7.2 11.4 %copy-start.7 = (s32[1,768]{1,0:T(1,128)S(1)}, s32[1,768]{1,0:T(1,128)}, u32[]{:S(2)}) copy-start(s32[1,768]{1,0:T(1,128)} %param.15) | copy-start | bytes 9220
  7.2 11.5 %copy-start.10 = (s32[1,4]{1,0:T(1,128)S(1)}, s32[1,4]{1,0:T(1,128)}, u32[]{:S(2)}) copy-start(s32[1,4]{1,0:T(1,128)} %param.14) | copy-start | bytes 52
  7.2 11.6 %copy-start.6 = (s32[1,768]{1,0:T(1,128)S(1)}, s32[1,768]{1,0:T(1,128)}, u32[]{:S(2)}) copy-start(s32[1,768]{1,0:T(1,128)} %param.16) | copy-start | bytes 9220
  7.2 11.6 %copy-start.8 = (f32[1,4,512]{2,1,0:T(4,128)S(1)}, f32[1,4,512]{2,1,0:T(4,128)}, u32[]{:S(2)}) copy-start(f32[1,4,512]{2,1,0:T(4,128)} %param.22) | copy-start | bytes 24580
  7.2 11.7 %copy-start.2 = (bf16[768,512]{1,0:T(8,128)(2,1)S(1)}, bf16[768,512]{1,0:T(8,128)(2,1)}, u32[]{:S(2)}) copy-start(bf16[768,512]{1,0:T(8,128)(2,1)} %param.13) | copy-start | bytes 2359300
  7.2 144.2 %all-reduce.3.cloned.1.call-start = ((), (), s32[]{:S(2)}) async-start(), calls=%async_computation | async-start | bytes 1048576 | tf_op jit(solution)/shard_map/psum | solution.py:118
  10.0 14.2 %copy-start.9 = (f32[1,2,512]{2,1,0:T(2,128)S(1)}, f32[1,2,512]{2,1,0:T(2,128)}, u32[]{:S(2)}) copy-start(f32[1,2,512]{2,1,0:T(2,128)} %param.23) | copy-start | bytes 12292
  10.0 23.1 %collective-permute-start = (bf16[4,128,512]{2,1,0:T(8,128)(2,1)}, bf16[4,128,512]{2,1,0:T(8,128)(2,1)}, u32[]{:S(2)}, u32[]{:S(2)}) collective-permute-start(bf16[4,128,512]{2,1,0:T(8,128)(2,1)} %get-tuple-element.15), channel_id=1, source_target_pairs={{0,4},{4,8},{8,12},{12,16},{16,20},{20,24},{24,28},{28,0},{1,5},{5... | collective-permute-start | bytes 1572872 | tf_op jit(solution)/shard_map/ppermute | solution.py:12
  11.3 25.3 %collective-permute-start.1 = (bf16[4,128,512]{2,1,0:T(8,128)(2,1)}, bf16[4,128,512]{2,1,0:T(8,128)(2,1)}, u32[]{:S(2)}, u32[]{:S(2)}) collective-permute-start(bf16[4,128,512]{2,1,0:T(8,128)(2,1)} %get-tuple-element.15), channel_id=1, source_target_pairs={{0,8},{4,12},{8,16},{12,20},{16,24},{20,28},{24,0},{28,4},{1,9},{5... | collective-permute-start | bytes 1572872 | tf_op jit(solution)/shard_map/ppermute | solution.py:12
  12.6 32.2 %collective-permute-start.2 = (bf16[4,128,512]{2,1,0:T(8,128)(2,1)}, bf16[4,128,512]{2,1,0:T(8,128)(2,1)}, u32[]{:S(2)}, u32[]{:S(2)}) collective-permute-start(bf16[4,128,512]{2,1,0:T(8,128)(2,1)} %get-tuple-element.15), channel_id=1, source_target_pairs={{0,12},{4,16},{8,20},{12,24},{16,28},{20,0},{24,4},{28,8},{1,13},{... | collective-permute-start | bytes 1572872 | tf_op jit(solution)/shard_map/ppermute | solution.py:12
  14.8 34.9 %collective-permute-start.3 = (bf16[4,128,512]{2,1,0:T(8,128)(2,1)}, bf16[4,128,512]{2,1,0:T(8,128)(2,1)}, u32[]{:S(2)}, u32[]{:S(2)}) collective-permute-start(bf16[4,128,512]{2,1,0:T(8,128)(2,1)} %get-tuple-element.15), channel_id=1, source_target_pairs={{0,28},{4,0},{8,4},{12,8},{16,12},{20,16},{24,20},{28,24},{1,29},{... | collective-permute-start | bytes 1572872 | tf_op jit(solution)/shard_map/ppermute | solution.py:12
  15.0 40.9 %collective-permute-start.4 = (bf16[4,128,512]{2,1,0:T(8,128)(2,1)}, bf16[4,128,512]{2,1,0:T(8,128)(2,1)}, u32[]{:S(2)}, u32[]{:S(2)}) collective-permute-start(bf16[4,128,512]{2,1,0:T(8,128)(2,1)} %get-tuple-element.15), channel_id=1, source_target_pairs={{0,24},{4,28},{8,0},{12,4},{16,8},{20,12},{24,16},{28,20},{1,25},{... | collective-permute-start | bytes 1572872 | tf_op jit(solution)/shard_map/ppermute | solution.py:12
  33.1 50.3 %collective-permute-start.5 = (bf16[4,128,512]{2,1,0:T(8,128)(2,1)}, bf16[4,128,512]{2,1,0:T(8,128)(2,1)S(1)}, u32[]{:S(2)}, u32[]{:S(2)}) collective-permute-start(bf16[4,128,512]{2,1,0:T(8,128)(2,1)} %get-tuple-element.15), channel_id=1, source_target_pairs={{0,20},{4,24},{8,28},{12,0},{16,4},{20,8},{24,12},{28,16},{1,21},{... | collective-permute-start | bytes 1572872 | tf_op jit(solution)/shard_map/ppermute | solution.py:12
  91.0 8.3 %copy-start.4 = (f32[768,512]{1,0:T(8,128)S(1)}, f32[768,512]{1,0:T(8,128)}, u32[]{:S(2)}) copy-start(f32[768,512]{1,0:T(8,128)} %fusion.23) | copy-start | bytes 4718596
  107.4 1.4 copy-start.3
  108.8 2.7 %copy-start.5 = (f32[4,128,512]{2,1,0:T(8,128)S(1)}, f32[4,128,512]{2,1,0:T(8,128)}, u32[]{:S(2)}) copy-start(f32[4,128,512]{2,1,0:T(8,128)} %fusion.20) | copy-start | bytes 3145732
Sparse Core Ops, SparseCore 0:
  115.4 36.0 all-reduce.2
where the time goes:
time: 163 us; the launch traced here: 160 us
  waiting for transfers between devices  76 us (47%)
  local copies, waits for them, and re-layouts  33.9 us (21%)
  matrix products  22.8 us (14%)
  between operations  14.9 us (9%)
  starting transfers between devices  8.09 us (5%)
  other arithmetic  4.44 us (3%)
    ppermute x6, waiting for transfers between devices, from_behind(): return lax.ppermute(value, axis, pairs)  39.8 us
    psum x1, waiting for transfers between devices, local(): lax.psum((jnp.sum(finals, axis=0), jnp.sum(finals * finals, axis=0)), 'me...  36.2 us
    unnamed x27, local copies, waits for them, and re-layouts  9.88 us
    gather x1, local copies, waits for them, and re-layouts, local(): senders = jnp.take(row_table, row_index, axis=1)  8.27 us
    dot_general x1, matrix products, edge_update(): jnp.einsum('mel,lk->mek', activated, weight_out, preferred_element_type=j...  8.12 us
    ppermute x6, starting transfers between devices, from_behind(): return lax.ppermute(value, axis, pairs)  8.05 us
    concatenate x2, local copies, waits for them, and re-layouts, local(): row_table = jnp.concatenate(pieces, axis=1)  7.63 us
    gather x1, local copies, waits for them, and re-layouts, local(): dest_proj = jnp.take(receiver_proj, dst_node, axis=1)  6.04 us
  transfers between devices with their start and end apart: 7, of which 6 were waited for; matrix products, arithmetic and copies ran while one was open for 15% of the time, Pallas kernels for 0%

commit v1 on v0

v1 whole, which is shorter than its diff:
```python
import functools

import jax
import jax.numpy as jnp
from jax import lax
from jax.experimental import pallas as pl
from jax.experimental.pallas import tpu as pltpu
from jax.sharding import PartitionSpec as P

RADIUS = 3
CAP = 32
REACH = 2 * RADIUS
MESH = pl.DeviceIdType.MESH
F32 = jnp.float32
BF16 = jnp.bfloat16


def dot(a, b):
    return jnp.dot(a, b, preferred_element_type=F32)


def silu(v):
    h = 0.5 * v
    return h * jnp.tanh(h) + h


def layer_norm(values, gain):
    centre = jnp.mean(values, axis=-1, keepdims=True)
    centered = values - centre
    variance = jnp.mean(centered * centered, axis=-1, keepdims=True)
    return centered * lax.rsqrt(variance + 1e-05) * gain


def kernel(
    groups,
    peers,
    nbr_ref,
    count_ref,
    src_ref,
    dst_ref,
    bias_ref,
    gain_ref,
    x_hbm,
    edge_hbm,
    ein_hbm,
    eout_hbm,
    nin_hbm,
    nout_hbm,
    out_ref,
    x,
    edge,
    ein,
    eout,
    nin,
    nout,
    ask,
    asked,
    outbox,
    table,
    hot,
    dest_hot,
    edge_proj,
    node_proj,
    finals,
    inbox,
    load_sem,
    ask_send,
    ask_recv,
    row_send,
    row_recv,
    fin_send,
    fin_recv,
    res_send,
    res_recv,
):
    members, rows, width = x.shape
    slots = edge.shape[0]
    nbrs = nbr_ref.shape[1]
    part = rows // peers
    me_g = lax.axis_index("graph")
    me_m = lax.axis_index("member")
    steps = [r + 1 for r in range(RADIUS)] + [-(r + 1) for r in range(RADIUS)]

    def ahead(step):
        return lax.rem(me_g + step + groups, groups)

    def peer(k):
        return lax.rem(me_m + k, peers)

    loads = [
        pltpu.make_async_copy(s, d, load_sem.at[i])
        for i, (s, d) in enumerate(
            [
                (x_hbm, x),
                (ein_hbm.at[0, 1], ein.at[1]),
                (ein_hbm.at[0, 2], ein.at[2]),
                (edge_hbm, edge),
                (ein_hbm.at[0, 0], ein.at[0]),
                (nin_hbm.at[0], nin),
                (eout_hbm.at[0], eout),
                (nout_hbm.at[0], nout),
            ]
        )
    ]
    for load in loads:
        load.start()

    barrier = pltpu.get_barrier_semaphore()
    for step in steps:
        pl.semaphore_signal(
            barrier, inc=1, device_id=(ahead(step), me_m), device_id_type=MESH
        )
    for k in range(1, peers):
        pl.semaphore_signal(
            barrier, inc=1, device_id=(me_g, peer(k)), device_id_type=MESH
        )

    src = src_ref[...]
    dst = dst_ref[...]
    live = lax.broadcasted_iota(jnp.int32, (1, slots), 1) < count_ref[0]
    slot = jnp.zeros_like(src)
    for k in range(1, nbrs + 1):
        slot = slot + (src >= k * rows).astype(jnp.int32)
    node = src - slot * rows
    owner = jnp.zeros_like(src)
    for k in range(nbrs):
        owner = jnp.where(slot == k, nbr_ref[0, k], owner)
    distance = me_g - owner
    distance = jnp.where(distance < 0, distance + groups, distance)
    distance = jnp.where((slot < nbrs) & live, distance, -1)
    place = lax.broadcasted_iota(jnp.int32, (8, slots), 0)
    wanted = jnp.where(place < RADIUS, place + 1, groups - (place - (RADIUS - 1)))
    wanted = jnp.where(place < REACH, wanted, -2)
    from_place = (jnp.broadcast_to(distance, (8, slots)) == wanted).astype(F32)
    node_hot = (
        lax.broadcasted_iota(jnp.int32, (rows, slots), 0)
        == jnp.broadcast_to(node, (rows, slots))
    ).astype(F32).astype(BF16)
    uses = lax.dot_general(
        from_place.astype(BF16),
        node_hot,
        (((1,), (1,)), ((), ())),
        preferred_element_type=F32,
    )
    need = jnp.minimum(uses, 1.0)
    for p in range(REACH):
        ask[p] = jnp.broadcast_to(need[p : p + 1, :], (8, rows))

    pl.semaphore_wait(barrier, REACH + peers - 1)

    def ask_copy(p):
        return pltpu.make_async_remote_copy(
            src_ref=ask.at[p],
            dst_ref=asked.at[p],
            send_sem=ask_send.at[p],
            recv_sem=ask_recv.at[p],
            device_id=(ahead(-steps[p]), me_m),
            device_id_type=MESH,
        )

    for p in range(REACH):
        ask_copy(p).start()

    before = (
        lax.broadcasted_iota(jnp.int32, (rows, rows), 0)
        < lax.broadcasted_iota(jnp.int32, (rows, rows), 1)
    ).astype(F32).astype(BF16)

    loads[0].wait()
    loads[1].wait()
    states = x[...].reshape(members * rows, width)
    table[:, :rows, :] = (
        dot(states, ein[1]).astype(BF16).reshape(members, rows, width)
    )

    for p in range(REACH):
        ask_copy(p).wait_recv()
    picks = []
    for p in range(REACH):
        got = asked[p]
        rank = dot(got.astype(BF16), before)
        order = lax.broadcasted_iota(jnp.int32, (CAP, rows), 0).astype(F32)
        pick = (jnp.broadcast_to(rank[:1], (CAP, rows)) == order) & (
            jnp.broadcast_to(got[:1], (CAP, rows)) > 0.0
        )
        picks.append(pick.astype(F32).astype(BF16))
    picks = jnp.concatenate(picks, axis=0)

    def row_copy(m, p):
        return pltpu.make_async_remote_copy(
            src_ref=outbox.at[m, p],
            dst_ref=table.at[m, pl.ds(2 * rows + p * CAP, CAP)],
            send_sem=row_send.at[m, p],
            recv_sem=row_recv.at[m, p],
            device_id=(ahead(steps[p]), me_m),
            device_id_type=MESH,
        )

    for m in range(members):
        outbox[m] = dot(picks, table[m, :rows, :]).astype(BF16).reshape(REACH, CAP, width)
        for p in range(REACH):
            row_copy(m, p).start()

    loads[2].wait()
    table[:, rows : 2 * rows, :] = (
        dot(states, ein[2]).astype(BF16).reshape(members, rows, width)
    )
    tail = 2 * rows + REACH * CAP
    table[:, tail:, :] = jnp.zeros((members, table.shape[1] - tail, width), BF16)
    ranks = dot(need.astype(BF16), before).astype(BF16)
    rank = jnp.sum(dot(ranks, node_hot) * from_place, axis=0, keepdims=True)
    at_place = jnp.sum(from_place * place.astype(F32), axis=0, keepdims=True)
    target = jnp.where(
        slot == nbrs, node.astype(F32), 2.0 * rows + at_place * CAP + rank
    )
    lanes = 128
    target = jnp.broadcast_to(target, (lanes, slots)).T
    receiver = jnp.broadcast_to(dst.astype(F32) + rows, (lanes, slots)).T
    column = lax.broadcasted_iota(jnp.int32, (slots, lanes), 1).astype(F32)
    for s in range(table.shape[1] // lanes):
        column_s = column + float(s * lanes)
        hit = (target == column_s) | (receiver == column_s)
        hot[:, s * lanes : (s + 1) * lanes] = hit.astype(F32).astype(BF16)
    dest_hot[...] = (
        (
            lax.broadcasted_iota(jnp.int32, (rows, slots), 0)
            == jnp.broadcast_to(dst, (rows, slots))
        )
        & jnp.broadcast_to(live, (rows, slots))
    ).astype(F32).astype(BF16)
    loads[3].wait()
    loads[4].wait()
    edge_proj[...] = dot(edge[...], ein[0]) + bias_ref[0, 0:1, :]
    loads[5].wait()
    node_proj[...] = (dot(states, nin[0]) + bias_ref[0, 2:3, :]).reshape(
        members, rows, width
    )
    loads[6].wait()
    loads[7].wait()

    def fin_copy(m, k):
        return pltpu.make_async_remote_copy(
            src_ref=finals.at[m, pl.ds(pl.multiple_of(peer(k) * part, part), part)],
            dst_ref=inbox.at[k - 1, m],
            send_sem=fin_send.at[m, k - 1],
            recv_sem=fin_recv.at[m, k - 1],
            device_id=(me_g, peer(k)),
            device_id_type=MESH,
        )

    chunk = slots // 3

    def one_member(m, carry):
        for p in range(REACH):
            row_copy(m, p).wait_recv()
        total = jnp.zeros((rows, width), F32)
        for c in range(0, slots, chunk):
            hidden = dot(hot[c : c + chunk, :], table[m]) + edge_proj[c : c + chunk, :]
            mixed = dot(silu(hidden).astype(BF16), eout[...]) + bias_ref[0, 1:2, :]
            updated = edge[c : c + chunk, :].astype(F32) + layer_norm(
                mixed, gain_ref[0, 0:1, :]
            )
            total = total + dot(dest_hot[:, c : c + chunk], updated.astype(BF16))
        hidden = node_proj[m] + dot(total.astype(BF16), nin[1])
        mixed = dot(silu(hidden).astype(BF16), nout[...]) + bias_ref[0, 3:4, :]
        final = x[m].astype(F32) + layer_norm(mixed, gain_ref[0, 1:2, :])
        finals[m] = final.astype(BF16)
        for k in range(1, peers):
            fin_copy(m, k).start()
        return carry

    lax.fori_loop(0, members, one_member, 0)

    for m in range(members):
        for k in range(1, peers):
            fin_copy(m, k).wait_recv()
    mine = pl.ds(pl.multiple_of(me_m * part, part), part)
    ensemble = members * peers
    parts = [finals[m, mine, :] for m in range(members)]
    parts += [inbox[k, m] for k in range(peers - 1) for m in range(members)]
    total = parts[0].astype(F32)
    for value in parts[1:]:
        total = total + value.astype(F32)
    centre = total * (1.0 / ensemble)
    square = jnp.zeros_like(centre)
    for value in parts:
        deviation = value.astype(F32) - centre
        square = square + deviation * deviation
    out_ref[0, mine, :] = centre.astype(BF16)
    out_ref[1, mine, :] = jnp.sqrt(square * (1.0 / ensemble)).astype(BF16)

    def res_copy(i, k):
        return pltpu.make_async_remote_copy(
            src_ref=out_ref.at[i, mine],
            dst_ref=out_ref.at[i, mine],
            send_sem=res_send.at[i, k - 1],
            recv_sem=res_recv.at[i, k - 1],
            device_id=(me_g, peer(k)),
            device_id_type=MESH,
        )

    for k in range(1, peers):
        for i in range(2):
            res_copy(i, k).start()
    for k in range(1, peers):
        for i in range(2):
            res_copy(i, k).wait()
    for p in range(REACH):
        ask_copy(p).wait_send()
        for m in range(members):
            row_copy(m, p).wait_send()
    for k in range(1, peers):
        for m in range(members):
            fin_copy(m, k).wait_send()


def local(
    node_latents,
    edge_latents,
    neighbours,
    edge_source,
    edge_dest,
    edge_count,
    edge_in,
    edge_out,
    node_in,
    node_out,
    biases,
    gains,
):
    members, rows, width = node_latents.shape
    slots = edge_source.shape[1]
    groups = lax.axis_size("graph")
    peers = lax.axis_size("member")
    part = rows // peers
    depth = 2 * rows + -(-(REACH * CAP) // 256) * 256
    vmem = pl.BlockSpec(memory_space=pltpu.VMEM)
    smem = pl.BlockSpec(memory_space=pltpu.SMEM)
    hbm = pl.BlockSpec(memory_space=pl.ANY)
    dma = pltpu.SemaphoreType.DMA
    both = pl.pallas_call(
        functools.partial(kernel, groups, peers),
        out_shape=jax.ShapeDtypeStruct((2, rows, width), BF16),
        in_specs=[smem, smem] + [vmem] * 4 + [hbm] * 6,
        out_specs=vmem,
        scratch_shapes=[
            pltpu.VMEM((members, rows, width), BF16),
            pltpu.VMEM((slots, width), BF16),
            pltpu.VMEM((3, width, width), BF16),
            pltpu.VMEM((width, width), BF16),
            pltpu.VMEM((2, width, width), BF16),
            pltpu.VMEM((width, width), BF16),
            pltpu.VMEM((REACH, 8, rows), F32),
            pltpu.VMEM((REACH, 8, rows), F32),
            pltpu.VMEM((members, REACH, CAP, width), BF16),
            pltpu.VMEM((members, depth, width), BF16),
            pltpu.VMEM((slots, depth), BF16),
            pltpu.VMEM((rows, slots), BF16),
            pltpu.VMEM((slots, width), F32),
            pltpu.VMEM((members, rows, width), F32),
            pltpu.VMEM((members, rows, width), BF16),
            pltpu.VMEM((peers - 1, members, part, width), BF16),
            dma((8,)),
            dma((REACH,)),
            dma((REACH,)),
            dma((members, REACH)),
            dma((members, REACH)),
            dma((members, peers - 1)),
            dma((members, peers - 1)),
            dma((2, peers - 1)),
            dma((2, peers - 1)),
        ],
        compiler_params=pltpu.CompilerParams(collective_id=0, has_side_effects=True),
    )(
        neighbours,
        edge_count,
        edge_source,
        edge_dest,
        biases,
        gains,
        node_latents,
        edge_latents,
        edge_in,
        edge_out,
        node_in,
        node_out,
    )
    return (both[0], both[1])


def solution(mesh):
    return jax.shard_map(
        local,
        mesh=mesh,
        in_specs=(
            P("member", "graph", None),
            P("graph", None),
            P("graph", None),
            P("graph", None),
            P("graph", None),
            P("graph"),
            P(),
            P(),
            P(),
            P(),
            P(),
            P(),
        ),
        out_specs=(P("graph", None), P("graph", None)),
        check_vma=False,
    )
```

time: 163 us -> 43.9 us (0.27); the launches traced: 160 us -> 43.7 us
  waiting for transfers between devices: 76 us -> 0 us
  Pallas kernels: 0 us -> 40.7 us
  local copies, waits for them, and re-layouts: 33.9 us -> 1.68 us
  matrix products: 22.8 us -> 0 us
  between operations: 14.9 us -> 1.29 us
  starting transfers between devices: 8.09 us -> 0 us
  other arithmetic: 4.44 us -> 0 us
    pallas_call x0 -> x1, Pallas kernels: none -> 40.7 us  [local(): pl.pallas_call(functools.partial(kernel, groups, peers), out_shape=jax.Sh...]
    ppermute x6 -> x0, waiting for transfers between devices: 39.8 us -> none  [from_behind(): return lax.ppermute(value, axis, pairs)]
    psum x1 -> x0, waiting for transfers between devices: 36.2 us -> none  [local(): lax.psum((jnp.sum(finals, axis=0), jnp.sum(finals * finals, axis=0)), 'me...]
    dot_general x7 -> x0, matrix products: 22.8 us -> none  [the longest x1 8.12 us: edge_update(): jnp.einsum('mel,lk->mek', activated, weight_out, preferred_element_type=j...]
    gather x2 -> x0, local copies, waits for them, and re-layouts: 14.3 us -> none  [the longest x1 8.27 us: local(): senders = jnp.take(row_table, row_index, axis=1)]
    unnamed x27 -> x0, local copies, waits for them, and re-layouts: 9.88 us -> none
    ppermute x6 -> x0, starting transfers between devices: 8.05 us -> none  [from_behind(): return lax.ppermute(value, axis, pairs)]
    concatenate x2 -> x0, local copies, waits for them, and re-layouts: 7.63 us -> none  [local(): row_table = jnp.concatenate(pieces, axis=1)]
  transfers between devices with their start and end apart: 7 -> 0, of which waited for: 6 -> 0; matrix products, arithmetic and copies ran while one was open for 15% -> 0% of each run, Pallas kernels for 0% -> 0%
where the time goes in v1:
time: 43.9 us; the launch traced here: 43.7 us
  Pallas kernels  40.7 us (93%)
  local copies, waits for them, and re-layouts  1.68 us (4%)
  between operations  1.29 us (3%)
    pallas_call x1, Pallas kernels, local(): pl.pallas_call(functools.partial(kernel, groups, peers), out_shape=jax.Sh...  40.7 us
    squeeze x1, local copies, waits for them, and re-layouts, local(): return (both[0], both[1])  1.68 us

profile of v1, /device:TPU:5, one launch (start us, length us, event | category | flops | bytes accessed | tf_op | source)
XLA Modules:
  0.0 43.7 jit_solution(3195429093779751579)
XLA Ops:
  1.3 40.7 %shard_map.131 = bf16[2,128,512]{2,1,0:T(8,128)(2,1)} custom-call(s32[1,4]{1,0:T(1,128)} %nbr_ref.1, s32[1]{0:T(128)S(6)} %copy.14.count_ref, s32[1,768]{1,0:T(1,128)} %src_ref.1, s32[1,768]{1,0:T(1,128)} %dst_ref.1, f32[1,4,512]{2,1,0:T(4,128)} %bias_ref.1, f32[1,2,512]{2,1,0:T(2,128)} %gain_ref.1, bf16[4,128,512]{2,1,0:T(8,128)(2,1)} %x_hbm.1, ...), custom_call_target="tpu_custom_call" | custom-call | tf_op jit(solution)/shard_map/pallas_call | solution.py:341
  42.0 1.7 %slice_bitcast_fusion = (bf16[128,512]{1,0:T(8,128)(2,1)}, bf16[128,512]{1,0:T(8,128)(2,1)}) fusion(bf16[2,128,512]{2,1,0:T(8,128)(2,1)} %shard_map.131), kind=kLoop, calls=%fused_computation | loop fusion | bytes 524288 | tf_op jit(solution)/shard_map/squeeze | solution.py:388

commit v2 on v1

--- a/solution.py
+++ b/solution.py
@@ -76,7 +76,8 @@
     members, rows, width = x.shape
     slots = edge.shape[0]
     nbrs = nbr_ref.shape[1]
-    part = rows // peers
+    part = inbox.shape[2]
+    pair = rows // part
     me_g = lax.axis_index("graph")
     me_m = lax.axis_index("member")
     steps = [r + 1 for r in range(RADIUS)] + [-(r + 1) for r in range(RADIUS)]
@@ -238,9 +239,12 @@
     loads[6].wait()
     loads[7].wait()
 
+    def share(device):
+        return pl.ds(pl.multiple_of(lax.rem(device, pair) * part, part), part)
+
     def fin_copy(m, k):
         return pltpu.make_async_remote_copy(
-            src_ref=finals.at[m, pl.ds(pl.multiple_of(peer(k) * part, part), part)],
+            src_ref=finals.at[m, share(peer(k))],
             dst_ref=inbox.at[k - 1, m],
             send_sem=fin_send.at[m, k - 1],
             recv_sem=fin_recv.at[m, k - 1],
@@ -274,7 +278,8 @@
     for m in range(members):
         for k in range(1, peers):
             fin_copy(m, k).wait_recv()
-    mine = pl.ds(pl.multiple_of(me_m * part, part), part)
+    mine = share(me_m)
+    first = me_m - lax.rem(me_m, pair)
     ensemble = members * peers
     parts = [finals[m, mine, :] for m in range(members)]
     parts += [inbox[k, m] for k in range(peers - 1) for m in range(members)]
@@ -289,20 +294,23 @@
     out_ref[0, mine, :] = centre.astype(BF16)
     out_ref[1, mine, :] = jnp.sqrt(square * (1.0 / ensemble)).astype(BF16)
 
+    def mate(k):
+        return first + lax.rem(me_m - first + k, pair)
+
     def res_copy(i, k):
         return pltpu.make_async_remote_copy(
             src_ref=out_ref.at[i, mine],
             dst_ref=out_ref.at[i, mine],
             send_sem=res_send.at[i, k - 1],
             recv_sem=res_recv.at[i, k - 1],
-            device_id=(me_g, peer(k)),
+            device_id=(me_g, mate(k)),
             device_id_type=MESH,
         )
 
-    for k in range(1, peers):
+    for k in range(1, pair):
         for i in range(2):
             res_copy(i, k).start()
-    for k in range(1, peers):
+    for k in range(1, pair):
         for i in range(2):
             res_copy(i, k).wait()
     for p in range(REACH):
@@ -332,7 +340,8 @@
     slots = edge_source.shape[1]
     groups = lax.axis_size("graph")
     peers = lax.axis_size("member")
-    part = rows // peers
+    pair = 2 - peers % 2
+    part = rows // pair
     depth = 2 * rows + -(-(REACH * CAP) // 256) * 256
     vmem = pl.BlockSpec(memory_space=pltpu.VMEM)
     smem = pl.BlockSpec(memory_space=pltpu.SMEM)
@@ -367,8 +376,8 @@
             dma((members, REACH)),
             dma((members, peers - 1)),
             dma((members, peers - 1)),
-            dma((2, peers - 1)),
-            dma((2, peers - 1)),
+            dma((2, pair)),
+            dma((2, pair)),
         ],
         compiler_params=pltpu.CompilerParams(collective_id=0, has_side_effects=True),
     )(

time: 43.9 us -> 41.7 us (0.950)
  Pallas kernels: 40.7 us -> 38.6 us
    pallas_call x1, Pallas kernels: 40.7 us -> 38.6 us  [local(): pl.pallas_call(functools.partial(kernel, groups, peers), out_shape=jax.Sh...]
where the time goes in v2:
time: 41.7 us; the launch traced here: 41.5 us
  Pallas kernels  38.6 us (93%)
  local copies, waits for them, and re-layouts  1.68 us (4%)
  between operations  1.29 us (3%)
    pallas_call x1, Pallas kernels, local(): pl.pallas_call(functools.partial(kernel, groups, peers), out_shape=jax.Sh...  38.6 us
    squeeze x1, local copies, waits for them, and re-layouts, local(): return (both[0], both[1])  1.68 us

profile of v2, /device:TPU:5, one launch (start us, length us, event | category | flops | bytes accessed | tf_op | source)
XLA Modules:
  0.0 41.5 jit_solution(17127408235544514255)
XLA Ops:
  1.3 38.6 %shard_map.131 = bf16[2,128,512]{2,1,0:T(8,128)(2,1)} custom-call(s32[1,4]{1,0:T(1,128)} %nbr_ref.1, s32[1]{0:T(128)S(6)} %copy.14.count_ref, s32[1,768]{1,0:T(1,128)} %src_ref.1, s32[1,768]{1,0:T(1,128)} %dst_ref.1, f32[1,4,512]{2,1,0:T(4,128)} %bias_ref.1, f32[1,2,512]{2,1,0:T(2,128)} %gain_ref.1, bf16[4,128,512]{2,1,0:T(8,128)(2,1)} %x_hbm.1, ...), custom_call_target="tpu_custom_call" | custom-call | tf_op jit(solution)/shard_map/pallas_call | solution.py:350
  39.9 1.7 %slice_bitcast_fusion = (bf16[128,512]{1,0:T(8,128)(2,1)}, bf16[128,512]{1,0:T(8,128)(2,1)}) fusion(bf16[2,128,512]{2,1,0:T(8,128)(2,1)} %shard_map.131), kind=kLoop, calls=%fused_computation | loop fusion | bytes 524288 | tf_op jit(solution)/shard_map/squeeze | solution.py:397

commit v3 on v2

--- a/solution.py
+++ b/solution.py
@@ -10,6 +10,7 @@
 RADIUS = 3
 CAP = 32
 REACH = 2 * RADIUS
+WAVES = ((0, 1, 2, 3, 4, 5),)
 MESH = pl.DeviceIdType.MESH
 F32 = jnp.float32
 BF16 = jnp.bfloat16
@@ -103,9 +104,6 @@
             ]
         )
     ]
-    for load in loads:
-        load.start()
-
     barrier = pltpu.get_barrier_semaphore()
     for step in steps:
         pl.semaphore_signal(
@@ -116,9 +114,12 @@
             barrier, inc=1, device_id=(me_g, peer(k)), device_id_type=MESH
         )
 
+    for load in loads:
+        load.start()
+
     src = src_ref[...]
     dst = dst_ref[...]
-    live = lax.broadcasted_iota(jnp.int32, (1, slots), 1) < count_ref[0]
+    live = lax.broadcasted_iota(jnp.int32, (1, slots), 1) < count_ref[0, 0]
     slot = jnp.zeros_like(src)
     for k in range(1, nbrs + 1):
         slot = slot + (src >= k * rows).astype(jnp.int32)
@@ -174,18 +175,15 @@
         dot(states, ein[1]).astype(BF16).reshape(members, rows, width)
     )
 
-    for p in range(REACH):
+    def picked(p):
         ask_copy(p).wait_recv()
-    picks = []
-    for p in range(REACH):
         got = asked[p]
         rank = dot(got.astype(BF16), before)
         order = lax.broadcasted_iota(jnp.int32, (CAP, rows), 0).astype(F32)
         pick = (jnp.broadcast_to(rank[:1], (CAP, rows)) == order) & (
             jnp.broadcast_to(got[:1], (CAP, rows)) > 0.0
         )
-        picks.append(pick.astype(F32).astype(BF16))
-    picks = jnp.concatenate(picks, axis=0)
+        return pick.astype(F32).astype(BF16)
 
     def row_copy(m, p):
         return pltpu.make_async_remote_copy(
@@ -197,10 +195,13 @@
             device_id_type=MESH,
         )
 
-    for m in range(members):
-        outbox[m] = dot(picks, table[m, :rows, :]).astype(BF16).reshape(REACH, CAP, width)
-        for p in range(REACH):
-            row_copy(m, p).start()
+    for places in WAVES:
+        picks = jnp.concatenate([picked(p) for p in places], axis=0)
+        for m in range(members):
+            drawn = dot(picks, table[m, :rows, :]).astype(BF16)
+            for i, p in enumerate(places):
+                outbox[m, p] = drawn[i * CAP : (i + 1) * CAP]
+                row_copy(m, p).start()
 
     loads[2].wait()
     table[:, rows : 2 * rows, :] = (
@@ -252,7 +253,7 @@
             device_id_type=MESH,
         )
 
-    chunk = slots // 3
+    chunk = slots
 
     def one_member(m, carry):
         for p in range(REACH):
@@ -382,7 +383,7 @@
         compiler_params=pltpu.CompilerParams(collective_id=0, has_side_effects=True),
     )(
         neighbours,
-        edge_count,
+        edge_count.reshape(1, 1),
         edge_source,
         edge_dest,
         biases,

time: 41.7 us -> 41.2 us (0.988); the launches traced: 41.5 us -> 40.5 us
  Pallas kernels: 38.6 us -> 37.5 us
    pallas_call x1, Pallas kernels: 38.6 us -> 37.5 us  [local(): pl.pallas_call(functools.partial(kernel, groups, peers), out_shape=jax.Sh...]
where the time goes in v3:
time: 41.2 us; the launch traced here: 40.5 us
  Pallas kernels  37.5 us (91%)
  local copies, waits for them, and re-layouts  1.68 us (4%)
  between operations  1.29 us (3%)
    pallas_call x1, Pallas kernels, local(): pl.pallas_call(functools.partial(kernel, groups, peers), out_shape=jax.Sh...  37.5 us
    squeeze x1, local copies, waits for them, and re-layouts, local(): return (both[0], both[1])  1.68 us

profile of v3, /device:TPU:5, one launch (start us, length us, event | category | flops | bytes accessed | tf_op | source)
XLA Modules:
  0.0 40.5 jit_solution(18043782227960040874)
XLA Ops:
  1.3 37.5 %shard_map.131 = bf16[2,128,512]{2,1,0:T(8,128)(2,1)} custom-call(s32[1,4]{1,0:T(1,128)} %nbr_ref.1, s32[1,1]{1,0:T(1,128)} %bitcast.5.count_ref, s32[1,768]{1,0:T(1,128)} %src_ref.1, s32[1,768]{1,0:T(1,128)} %dst_ref.1, f32[1,4,512]{2,1,0:T(4,128)} %bias_ref.1, f32[1,2,512]{2,1,0:T(2,128)} %gain_ref.1, bf16[4,128,512]{2,1,0:T(8,128)(2,1)} %x_hbm.1, ...), custom_call_target="tpu_custom_call" | custom-call | tf_op jit(solution)/shard_map/pallas_call | solution.py:351
  38.8 1.7 %slice_bitcast_fusion = (bf16[128,512]{1,0:T(8,128)(2,1)}, bf16[128,512]{1,0:T(8,128)(2,1)}) fusion(bf16[2,128,512]{2,1,0:T(8,128)(2,1)} %shard_map.131), kind=kLoop, calls=%fused_computation | loop fusion | bytes 524288 | tf_op jit(solution)/shard_map/squeeze | solution.py:398
